TPU v7x, 32 devices: a whole 2x2x4 slice. The times are simulated.
32 devices in a mesh: dp: 4 (over y, x), seq: 4 (over z), grp: 2 (over core).
Axes of the slice: x: 2, y: 2, z: 4, core: 2. Of those that a mesh axis runs over, the one named last changes fastest.
Arguments:
- text_proj: bfloat16 [3, 16, 12, 128, 128], P(None, 'dp', None, ('seq', 'grp')), may hold values from -50 to 50
- image_proj: bfloat16 [3, 16, 12, 160, 128], P(None, ('dp', 'seq'), None, 'grp'), may hold values from -50 to 50
- text_grad: bfloat16 [16, 12, 128, 128], P('dp', None, ('seq', 'grp')), may hold values from -15 to 15
- image_grad: bfloat16 [16, 12, 160, 128], P(('dp', 'seq'), None, 'grp'), may hold values from -15 to 15
- text_lengths: int32 [16], P(('dp', 'seq')), may hold values from 1 to 128
- norm_gains: float32 [2, 2, 128], replicated, may hold values from 0.7 to 5.2
Outputs:
- text_out: bfloat16 [16, 12, 128, 128], P('dp', None, ('seq', 'grp'))
- image_out: bfloat16 [16, 12, 160, 128], P(('dp', 'seq'), None, 'grp')
- text_proj_grad: bfloat16 [3, 16, 12, 128, 128], P(None, 'dp', None, ('seq', 'grp'))
- image_proj_grad: bfloat16 [3, 16, 12, 160, 128], P(None, ('dp', 'seq'), None, 'grp')
- gain_grad: float32 [2, 2, 128], replicated
All inputs are finite; a program needn't handle non-finite values.
Results may differ from a plain program's by a relative error of at most 0.025.
The roundings to bfloat16 on the way count: a program that leaves them out, or rounds other values in their place, can miss the bound.
Values may be sent and summed in bfloat16 or wider, within the bound.
No kernel may reach another device: no remote copies, remote signals or barrier semaphores. Data moves between devices by JAX's collectives and lax.ppermute only.
A program may use at most 64 MiB of HBM per device.

v0:
```python
import jax
import jax.numpy as jnp
from jax import lax
from jax.sharding import PartitionSpec as P

TXT = 128
EPSILON = 1e-06
MASKED = -1e30


def forward(queries, key_rows, value_rows, key_valid):
    factor = queries.shape[-1] ** (-0.5)
    scores = (
        jnp.einsum("nqd,nkd->nqk", queries, key_rows, preferred_element_type=jnp.float32) * factor
    )
    scores = jnp.where(key_valid[:, None, :], scores, MASKED)
    row_max = jnp.max(scores, axis=-1, keepdims=True)
    exponent = jnp.exp(scores - row_max)
    attn_probs = exponent / jnp.sum(exponent, axis=-1, keepdims=True)
    rounded_probs = attn_probs.astype(jnp.bfloat16)
    attn_local = jnp.einsum(
        "nqk,nkd->nqd", rounded_probs, value_rows, preferred_element_type=jnp.float32
    )
    return (attn_probs, rounded_probs, attn_local)


def backward_terms(queries, key_rows, value_rows, attn_probs, rounded_probs, grad_out):
    factor = queries.shape[-1] ** (-0.5)
    grad_value = jnp.einsum(
        "nqk,nqd->nkd", rounded_probs, grad_out, preferred_element_type=jnp.float32
    )
    grad_probs = jnp.einsum(
        "nqd,nkd->nqk", grad_out, value_rows, preferred_element_type=jnp.float32
    )
    row_delta = jnp.sum(attn_probs * grad_probs, axis=-1, keepdims=True)
    grad_scores = (attn_probs * (grad_probs - row_delta) * factor).astype(jnp.bfloat16)
    grad_query = jnp.einsum(
        "nqk,nkd->nqd", grad_scores, key_rows, preferred_element_type=jnp.float32
    ).astype(jnp.bfloat16)
    grad_key = jnp.einsum("nqk,nqd->nkd", grad_scores, queries, preferred_element_type=jnp.float32)
    return (grad_query, grad_key, grad_value)


def sums_item(packed):
    query_one, key_one, value_one, valid_one, grad_one = packed
    attn_probs, rounded_probs, attn_local = forward(
        query_one[None], key_one[None], value_one[None], valid_one[None]
    )
    grad_query, grad_key, grad_value = backward_terms(
        query_one[None], key_one[None], value_one[None], attn_probs, rounded_probs, grad_one[None]
    )
    return (attn_local[0].astype(jnp.bfloat16), grad_query[0], grad_key[0], grad_value[0])


def whole_item(packed):
    attn_local, grad_query, grad_key, grad_value = sums_item(packed)
    return (attn_local, grad_query, grad_key.astype(jnp.bfloat16), grad_value.astype(jnp.bfloat16))


def unit_parts(raw_bf):
    raw_vals = raw_bf.astype(jnp.float32)
    inverse = lax.rsqrt(jnp.mean(raw_vals * raw_vals, axis=-1, keepdims=True) + EPSILON)
    return (raw_vals * inverse, inverse)


def raw_gradient(grad_normed_bf, unit_vec, inverse, gain_rows):
    grad_normed = grad_normed_bf.astype(jnp.float32)
    gain_part = jnp.sum(grad_normed * unit_vec, axis=(1, 2, 3))
    grad_unit = grad_normed * gain_rows
    grad_raw = inverse * (
        grad_unit - unit_vec * jnp.mean(grad_unit * unit_vec, axis=-1, keepdims=True)
    )
    return (grad_raw.astype(jnp.bfloat16), gain_part)


def global_position(local_row, owner_index, text_rows, text_group, image_rows, grp_count):
    text_place = (
        local_row // text_group * grp_count + owner_index
    ) * text_group + local_row % text_group
    image_place = TXT + owner_index * image_rows + (local_row - text_rows)
    return jnp.where(local_row < text_rows, text_place, image_place)


def per_device(text_proj, image_proj, text_grad, image_grad, text_lengths, norm_gains):
    seq_count = lax.axis_size("seq")
    grp_count = lax.axis_size("grp")
    sample_count, head_count, image_rows, head_size = image_grad.shape
    text_group = text_proj.shape[3]
    text_rows = text_group * seq_count
    local_len = text_rows + image_rows
    text_unit, text_inverse = unit_parts(text_proj[:2])
    image_unit, image_inverse = unit_parts(image_proj[:2])
    text_gain = norm_gains[0][:, None, None, None, :]
    image_gain = norm_gains[1][:, None, None, None, :]
    text_stack = jnp.concatenate(
        [(text_unit * text_gain).astype(jnp.bfloat16), text_proj[2:]], axis=0
    )
    image_stack = jnp.concatenate(
        [(image_unit * image_gain).astype(jnp.bfloat16), image_proj[2:]], axis=0
    )
    text_here, text_cot = (
        lax.all_to_all(text_stack, "seq", split_axis=1, concat_axis=3, tiled=True),
        lax.all_to_all(text_grad[None], "seq", split_axis=1, concat_axis=3, tiled=True),
    )
    joint_rows = jnp.concatenate([text_here, image_stack], axis=3)
    cotangent_rows = jnp.concatenate([text_cot[0], image_grad], axis=2)
    key_row = jnp.arange(local_len * grp_count, dtype=jnp.int32)
    key_place = global_position(
        key_row % local_len, key_row // local_len, text_rows, text_group, image_rows, grp_count
    )
    key_valid = (key_place[None, :] >= TXT) | (key_place[None, :] < text_lengths[:, None])
    full_len = local_len * grp_count
    moved_rows, moved_cot = (
        lax.all_to_all(joint_rows, "grp", split_axis=2, concat_axis=3, tiled=True),
        lax.all_to_all(cotangent_rows[None], "grp", split_axis=2, concat_axis=3, tiled=True),
    )
    head_share = moved_rows.shape[2]
    item_count = sample_count * head_share
    flat_rows = moved_rows.reshape(3, item_count, full_len, head_size)
    item_valid = jnp.broadcast_to(
        key_valid[:, None, :], (sample_count, head_share, full_len)
    ).reshape(item_count, full_len)
    attn_local, grad_query, grad_key, grad_value = lax.map(
        whole_item,
        (
            flat_rows[0],
            flat_rows[1],
            flat_rows[2],
            item_valid,
            moved_cot.reshape(item_count, full_len, head_size),
        ),
    )
    results = jnp.stack([attn_local, grad_query, grad_key, grad_value]).reshape(
        4, sample_count, head_share, full_len, head_size
    )
    placed = lax.all_to_all(results, "grp", split_axis=3, concat_axis=2, tiled=True)
    text_back = lax.all_to_all(
        placed[:, :, :, :text_rows], "seq", split_axis=3, concat_axis=1, tiled=True
    )
    image_back = placed[:, :, :, text_rows:]
    text_raw, text_part = raw_gradient(text_back[1:3], text_unit, text_inverse, text_gain)
    image_raw, image_part = raw_gradient(image_back[1:3], image_unit, image_inverse, image_gain)
    partial_value = jnp.stack([text_part, image_part])
    summed_gain = lax.psum(partial_value, ("dp", "seq", "grp"))
    gain_grad = summed_gain / (sample_count * lax.axis_size("dp") * seq_count)
    text_proj_grad = jnp.concatenate([text_raw, text_back[3:]], axis=0)
    image_proj_grad = jnp.concatenate([image_raw, image_back[3:]], axis=0)
    return (text_back[0], image_back[0], text_proj_grad, image_proj_grad, gain_grad)


def solution(mesh):
    placed = (
        P(None, "dp", None, ("seq", "grp"), None),
        P(None, ("dp", "seq"), None, "grp", None),
        P("dp", None, ("seq", "grp"), None),
        P(("dp", "seq"), None, "grp", None),
        P(("dp", "seq")),
        P(),
    )
    return jax.shard_map(
        per_device,
        mesh=mesh,
        in_specs=placed,
        out_specs=(
            P("dp", None, ("seq", "grp"), None),
            P(("dp", "seq"), None, "grp", None),
            P(None, "dp", None, ("seq", "grp"), None),
            P(None, ("dp", "seq"), None, "grp", None),
            P(),
        ),
        check_vma=False,
    )
```

profile of v0, /device:TPU:10, one launch (start us, length us, event | category | flops | bytes accessed | tf_op | source)
XLA Modules:
  0.0 161.8 jit_solution(1333477667918705269)
XLA Ops:
  0.6 5.5 %all-to-all-start.2 = ((bf16[1,4,12,16,128]{4,3,2,0,1:T(8,128)(2,1)}), bf16[1,4,12,16,128]{4,3,2,0,1:T(8,128)(2,1)S(1)}, u32[]{:S(2)}, u32[]{:S(2)}) async-start(bf16[1,4,12,16,128]{4,3,2,0,1:T(8,128)(2,1)} %bitcast.157), calls=%async_computation.2 | async-start | bytes 393216 | tf_op jit(solution)/shard_map/all_to_all | solution.py:103
  6.8 1.3 fusion.56
  8.1 1.3 fusion.54
  12.1 4.1 %all_to_all.96 = bf16[1,1,12,144,128]{4,3,1,0,2:T(8,128)(2,1)S(1)} all-to-all(bf16[1,1,12,144,128]{4,3,1,0,2:T(8,128)(2,1)S(1)} %maximum_bitcast_fusion.1), channel_id=1, replica_groups=mesh['dp'=4,'seq'=4,'grp'=2] {'grp'}, dimensions={2} | all-to-all | bytes 884736 | tf_op jit(solution)/shard_map/all_to_all | solution.py:115
  16.2 5.0 %all-to-all-start = ((bf16[3,4,12,16,128]{4,3,2,0,1:T(8,128)(2,1)}), bf16[3,4,12,16,128]{4,3,2,0,1:T(8,128)(2,1)S(1)}, u32[]{:S(2)}, u32[]{:S(2)}) async-start(bf16[3,4,12,16,128]{4,3,2,0,1:T(8,128)(2,1)} %copy.85), calls=%async_computation | async-start | bytes 1179648 | tf_op jit(solution)/shard_map/all_to_all | solution.py:102
  23.0 11.4 %all-to-all-done = bf16[3,4,12,16,128]{4,3,2,0,1:T(8,128)(2,1)S(1)} async-done(((bf16[3,4,12,16,128]{4,3,2,0,1:T(8,128)(2,1)}), bf16[3,4,12,16,128]{4,3,2,0,1:T(8,128)(2,1)S(1)}, u32[]{:S(2)}, u32[]{:S(2)}) %all-to-all-start) | async-done | bytes 589856 | tf_op jit(solution)/shard_map/all_to_all | solution.py:102
  34.7 4.8 %all_to_all.97 = bf16[3,1,12,144,128]{4,3,1,0,2:T(8,128)(2,1)S(1)} all-to-all(bf16[3,1,12,144,128]{4,3,1,0,2:T(8,128)(2,1)S(1)} %maximum_maximum_fusion), channel_id=1, replica_groups=mesh['dp'=4,'seq'=4,'grp'=2] {'grp'}, dimensions={2} | all-to-all | bytes 2654208 | tf_op jit(solution)/shard_map/all_to_all | solution.py:114
  40.6 32.7 %while.16 = (s32[]{:T(128)}, bf16[6,288,128]{2,1,0:T(8,128)(2,1)}, bf16[6,288,128]{2,1,0:T(8,128)(2,1)}, bf16[6,288,128]{2,1,0:T(8,128)(2,1)}, bf16[6,288,128]{2...) while((s32[]{:T(128)}, bf16[6,288,128]{2,1,0:T(8,128)(2,1)}, ...), condition=%wide.region_6.7_spmd, body=%wide.region_2.6_spmd.sunk | while | flops 129290400 | bytes 4506681 | solution.py:123
  40.9 1.1 fusion.116
  43.0 1.1 multiply_reduce_fusion.2
  51.8 1.1 fusion.116
  57.3 1.1 fusion.116
  59.3 1.1 multiply_reduce_fusion.2
  62.7 1.1 fusion.116
  64.8 1.1 multiply_reduce_fusion.2
  68.2 1.1 fusion.116
  73.3 1.5 maximum_bitcast_fusion
  74.8 1.4 copy.95
  76.1 5.2 %all_to_all.98 = bf16[4,1,6,288,128]{4,0,2,1,3:T(4,128)(2,1)S(1)} all-to-all(bf16[4,1,6,288,128]{4,0,2,1,3:T(4,128)(2,1)S(1)} %copy.95), channel_id=1, replica_groups=mesh['dp'=4,'seq'=4,'grp'=2] {'grp'}, dimensions={3} | all-to-all | bytes 3538944 | tf_op jit(solution)/shard_map/all_to_all | solution.py:136
  81.7 1.6 copy.97
  83.3 7.5 %all-to-all-start.5 = ((bf16[4,1,12,64,128]{4,2,1,0,3:T(8,128)(2,1)}), bf16[4,1,12,64,128]{4,2,1,0,3:T(8,128)(2,1)}, u32[]{:S(2)}, u32[]{:S(2)}) async-start(bf16[4,1,12,64,128]{4,2,1,0,3:T(8,128)(2,1)} %copy.97), calls=%async_computation.5 | async-start | bytes 2097152 | tf_op jit(solution)/shard_map/all_to_all | solution.py:137
  94.0 19.8 %all-to-all-done.5 = bf16[4,1,12,64,128]{4,2,1,0,3:T(8,128)(2,1)} async-done(((bf16[4,1,12,64,128]{4,2,1,0,3:T(8,128)(2,1)}), bf16[4,1,12,64,128]{4,2,1,0,3:T(8,128)(2,1)}, u32[]{:S(2)}, u32[]{:S(2)}) %all-to-all-start.5) | async-done | bytes 786464 | tf_op jit(solution)/shard_map/all_to_all | solution.py:137
  113.8 1.7 %copy.98 = bf16[4,1,12,64,128]{4,3,2,0,1:T(8,128)(2,1)S(1)} copy(bf16[4,1,12,64,128]{4,2,1,0,3:T(8,128)(2,1)} %all-to-all-done.5) | data formatting | bytes 1572864 | tf_op jit(solution)/shard_map/all_to_all | solution.py:137
  116.1 42.8 %psum.7 = f32[2,2,128]{2,1,0:T(2,128)S(1)} all-reduce(f32[2,2,128]{2,1,0:T(2,128)S(1)} %pad_maximum_fusion.3), channel_id=1, replica_groups=mesh['dp'=4,'seq'=4,'grp'=2] {'dp','seq','grp'}, use_global_device_ids=true, to_apply=%region_11.12 | all-reduce | flops 512 | bytes 4096 | tf_op jit(solution)/shard_map/psum | solution.py:144
  (95 shorter events, 36.3 us)
Async XLA Ops:
  0.6 9.5 %copy-start.1 = (bf16[3,4,12,16,128]{4,3,2,1,0:T(8,128)(2,1)S(1)}, bf16[3,4,12,16,128]{4,3,2,1,0:T(8,128)(2,1)}, u32[]{:S(2)}) copy-start(bf16[3,4,12,16,128]{4,3,2,1,0:T(8,128)(2,1)} %param.8) | copy-start | bytes 1769476
  0.6 11.4 %all-to-all-start.2 = ((bf16[1,4,12,16,128]{4,3,2,0,1:T(8,128)(2,1)}), bf16[1,4,12,16,128]{4,3,2,0,1:T(8,128)(2,1)S(1)}, u32[]{:S(2)}, u32[]{:S(2)}) async-start(bf16[1,4,12,16,128]{4,3,2,0,1:T(8,128)(2,1)} %bitcast.157), calls=%async_computation.2 | async-start | bytes 393216 | tf_op jit(solution)/shard_map/all_to_all | solution.py:103
  8.1 4.0 %copy-start.3 = (bf16[1,12,80,128]{3,2,1,0:T(8,128)(2,1)S(1)}, bf16[1,12,80,128]{3,2,1,0:T(8,128)(2,1)}, u32[]{:S(2)}) copy-start(bf16[1,12,80,128]{3,2,1,0:T(8,128)(2,1)} %param.11) | copy-start | bytes 737284
  11.2 10.1 %copy-start = (bf16[3,1,12,80,128]{4,3,2,1,0:T(8,128)(2,1)S(1)}, bf16[3,1,12,80,128]{4,3,2,1,0:T(8,128)(2,1)}, u32[]{:S(2)}) copy-start(bf16[3,1,12,80,128]{4,3,2,1,0:T(8,128)(2,1)} %param.9) | copy-start | bytes 2211844
  16.2 18.2 %all-to-all-start = ((bf16[3,4,12,16,128]{4,3,2,0,1:T(8,128)(2,1)}), bf16[3,4,12,16,128]{4,3,2,0,1:T(8,128)(2,1)S(1)}, u32[]{:S(2)}, u32[]{:S(2)}) async-start(bf16[3,4,12,16,128]{4,3,2,0,1:T(8,128)(2,1)} %copy.85), calls=%async_computation | async-start | bytes 1179648 | tf_op jit(solution)/shard_map/all_to_all | solution.py:102
  39.5 1.0 copy-start.2
  83.3 30.5 %all-to-all-start.5 = ((bf16[4,1,12,64,128]{4,2,1,0,3:T(8,128)(2,1)}), bf16[4,1,12,64,128]{4,2,1,0,3:T(8,128)(2,1)}, u32[]{:S(2)}, u32[]{:S(2)}) async-start(bf16[4,1,12,64,128]{4,2,1,0,3:T(8,128)(2,1)} %copy.97), calls=%async_computation.5 | async-start | bytes 2097152 | tf_op jit(solution)/shard_map/all_to_all | solution.py:137
where the time goes:
time: 163 us; the launch traced here: 162 us
  blocking collectives  56.9 us (35%)
  waiting for transfers between devices  32.1 us (20%)
  matrix products  31 us (19%)
  starting transfers between devices  17.9 us (11%)
  local copies, waits for them, and re-layouts  12.2 us (7%)
  other arithmetic  9.94 us (6%)
    psum x1, blocking collectives, per_device(): summed_gain = lax.psum(partial_value, ('dp', 'seq', 'grp'))  42.8 us
    all_to_all x1, waiting for transfers between devices, per_device(): lax.all_to_all(placed[:, :, :, :text_rows], 'seq', split_axis=3, concat_a...  19.8 us
    all_to_all x1, waiting for transfers between devices, per_device(): lax.all_to_all(text_stack, 'seq', split_axis=1, concat_axis=3, tiled=True)  11.4 us
    all_to_all x1, starting transfers between devices, per_device(): lax.all_to_all(placed[:, :, :, :text_rows], 'seq', split_axis=3, concat_a...  7.47 us
    dot_general x6, matrix products, backward_terms(): jnp.einsum('nqk,nqd->nkd', rounded_probs, grad_out, preferred_element_typ...  6.74 us
    dot_general x6, matrix products, backward_terms(): jnp.einsum('nqd,nkd->nqk', grad_out, value_rows, preferred_element_type=j...  6.74 us
    dot_general x6, matrix products, forward(): jnp.einsum('nqk,nkd->nqd', rounded_probs, value_rows, preferred_element_t...  5.55 us
    all_to_all x1, starting transfers between devices, per_device(): lax.all_to_all(text_grad[None], 'seq', split_axis=1, concat_axis=3, tiled...  5.46 us
  transfers between devices with their start and end apart: 3, of which 3 were waited for; matrix products, arithmetic and copies ran while one was open for 6% of the time, Pallas kernels for 0%

commit v1 on v0

--- a/solution.py
+++ b/solution.py
@@ -6,6 +6,27 @@
 TXT = 128
 EPSILON = 1e-06
 MASKED = -1e30
+
+
+def create_the_steps_all(xs, array_axis, unit):
+    kept_arr = xs.shape
+    reply = jnp.moveaxis(
+        xs.reshape(
+            *kept_arr[:array_axis], unit, kept_arr[array_axis] // unit, *kept_arr[array_axis + 1 :]
+        ),
+        array_axis,
+        0,
+    )
+    return reply
+
+
+def _mark_entries(mine, dimension_no):
+    mine = jnp.moveaxis(mine, 0, dimension_no)
+    now = mine.shape
+    base_arr = mine.reshape(
+        *now[:dimension_no], now[dimension_no] * now[dimension_no + 1], *now[dimension_no + 2 :]
+    )
+    return base_arr
 
 
 def forward(queries, key_rows, value_rows, key_valid):
@@ -98,8 +119,27 @@
     image_stack = jnp.concatenate(
         [(image_unit * image_gain).astype(jnp.bfloat16), image_proj[2:]], axis=0
     )
+
+    def make_clusters_up(vector, axis_name, panel, xx):
+        item_now = lax.axis_index(axis_name)
+        far_arr = lax.axis_size(axis_name)
+        row_out, v_now = (far_arr, item_now)
+        e_next = create_the_steps_all(vector, panel, row_out)
+        seen_now = e_next
+        for rr in [*range(1, row_out)]:
+            z1, arr_now = ((v_now + rr) % row_out, (v_now - rr) % row_out)
+            found_now = lax.dynamic_index_in_dim(e_next, z1, 0)
+            next_value = lax.ppermute(
+                found_now,
+                axis_name=axis_name,
+                perm=[(kk, (kk + rr) % row_out) for kk in range(row_out)],
+            )
+            seen_now = lax.dynamic_update_slice_in_dim(seen_now, next_value, arr_now, axis=0)
+        arr_out = _mark_entries(seen_now, xx)
+        return arr_out
+
     text_here, text_cot = (
-        lax.all_to_all(text_stack, "seq", split_axis=1, concat_axis=3, tiled=True),
+        make_clusters_up(text_stack, "seq", 1, 3),
         lax.all_to_all(text_grad[None], "seq", split_axis=1, concat_axis=3, tiled=True),
     )
     joint_rows = jnp.concatenate([text_here, image_stack], axis=3)

time: 163 us -> 145 us (0.89)
  matrix products: 31 us -> 17 us
  local copies, waits for them, and re-layouts: 12.2 us -> 9.03 us
  waiting for transfers between devices: 32.1 us -> 30 us
  other arithmetic: 9.94 us -> 11.9 us
    all_to_all x1 -> x0, waiting for transfers between devices: 11.4 us -> none  [per_device(): lax.all_to_all(text_stack, 'seq', split_axis=1, concat_axis=3, tiled=True)]
    ppermute x0 -> x3, starting transfers between devices: none -> 6.47 us  [make_clusters_up(): lax.ppermute(found_now, axis_name=axis_name, perm=[(kk, (kk + rr) % row_o...]
    ppermute x0 -> x3, waiting for transfers between devices: none -> 5.62 us  [make_clusters_up(): lax.ppermute(found_now, axis_name=axis_name, perm=[(kk, (kk + rr) % row_o...]
    dot_general x6, matrix products: 6.74 us -> 1.47 us  [backward_terms(): jnp.einsum('nqk,nqd->nkd', rounded_probs, grad_out, preferred_element_typ...]
    dot_general x6, matrix products: 6.74 us -> 1.5 us  [backward_terms(): jnp.einsum('nqd,nkd->nqk', grad_out, value_rows, preferred_element_type=j...]
    all_to_all x1, waiting for transfers between devices: 0.88 us -> 5.97 us  [per_device(): lax.all_to_all(text_grad[None], 'seq', split_axis=1, concat_axis=3, tiled...]
    all_to_all x1 -> x0, starting transfers between devices: 5 us -> none  [per_device(): lax.all_to_all(text_stack, 'seq', split_axis=1, concat_axis=3, tiled=True)]
    dot_general x6, matrix products: 5.13 us -> 1.44 us  [backward_terms(): jnp.einsum('nqk,nqd->nkd', grad_scores, queries, preferred_element_type=j...]
  transfers between devices with their start and end apart: 3 -> 5, of which waited for: 3 -> 4; matrix products, arithmetic and copies ran while one was open for 6% -> 4% of each run, Pallas kernels for 0% -> 0%
where the time goes in v1:
time: 145 us; the launch traced here: 144 us
  blocking collectives  56.7 us (39%)
  waiting for transfers between devices  30 us (21%)
  starting transfers between devices  17.6 us (12%)
  matrix products  17 us (12%)
  other arithmetic  11.9 us (8%)
  local copies, waits for them, and re-layouts  9.03 us (6%)
  between operations  1.77 us (1%)
    psum x1, blocking collectives, per_device(): summed_gain = lax.psum(partial_value, ('dp', 'seq', 'grp'))  42.7 us
    all_to_all x1, waiting for transfers between devices, per_device(): lax.all_to_all(placed[:, :, :, :text_rows], 'seq', split_axis=3, concat_a...  18.4 us
    ppermute x3, starting transfers between devices, make_clusters_up(): lax.ppermute(found_now, axis_name=axis_name, perm=[(kk, (kk + rr) % row_o...  6.47 us
    all_to_all x1, starting transfers between devices, per_device(): lax.all_to_all(text_grad[None], 'seq', split_axis=1, concat_axis=3, tiled...  6.11 us
    all_to_all x1, waiting for transfers between devices, per_device(): lax.all_to_all(text_grad[None], 'seq', split_axis=1, concat_axis=3, tiled...  5.97 us
    ppermute x3, waiting for transfers between devices, make_clusters_up(): lax.ppermute(found_now, axis_name=axis_name, perm=[(kk, (kk + rr) % row_o...  5.62 us
    dot_general x6, matrix products, forward(): jnp.einsum('nqk,nkd->nqd', rounded_probs, value_rows, preferred_element_t...  5.55 us
    dot_general x6, matrix products, backward_terms(): jnp.einsum('nqk,nkd->nqd', grad_scores, key_rows, preferred_element_type=...  5.53 us
  transfers between devices with their start and end apart: 5, of which 4 were waited for; matrix products, arithmetic and copies ran while one was open for 4% of the time, Pallas kernels for 0%

profile of v1, /device:TPU:10, one launch (start us, length us, event | category | flops | bytes accessed | tf_op | source)
XLA Modules:
  0.0 144.1 jit_solution(8158529448860911546)
XLA Ops:
  0.7 1.3 fusion.56
  2.0 0.9 slice.62
  3.7 1.3 fusion.54
  5.6 1.6 %collective-permute-start = (bf16[1,3,1,12,16,128]{5,4,3,0,1,2:T(8,128)(2,1)S(1)}, bf16[1,3,1,12,16,128]{5,4,3,0,1,2:T(8,128)(2,1)S(1)}, u32[]{:S(2)}, u32[]{:S(2)}) collective-permute-start(bf16[1,3,1,12,16,128]{5,4,3,0,1,2:T(8,128)(2,1)S(1)} %get-tuple-element.120), channel_id=1, source_target_pairs={{0,2},{2,4},{4,6},{6,0},{1,3},{3,5},{5,7},{7,1},{8,10},{10,12},{12... | collective-permute-start | bytes 442376 | tf_op jit(solution)/shard_map/ppermute | solution.py:132
  7.2 4.4 %collective-permute-start.1 = (bf16[1,3,1,12,16,128]{5,4,3,0,1,2:T(8,128)(2,1)S(1)}, bf16[1,3,1,12,16,128]{5,4,3,0,1,2:T(8,128)(2,1)S(1)}, u32[]{:S(2)}, u32[]{:S(2)}) collective-permute-start(bf16[1,3,1,12,16,128]{5,4,3,0,1,2:T(8,128)(2,1)S(1)} %get-tuple-element.121), channel_id=1, source_target_pairs={{0,4},{2,6},{4,0},{6,2},{1,5},{3,7},{5,1},{7,3},{8,12},{10,14},{12... | collective-permute-start | bytes 442376 | tf_op jit(solution)/shard_map/ppermute | solution.py:132
  13.8 3.2 %collective-permute-done = bf16[1,3,1,12,16,128]{5,4,3,0,1,2:T(8,128)(2,1)S(1)} collective-permute-done((bf16[1,3,1,12,16,128]{5,4,3,0,1,2:T(8,128)(2,1)S(1)}, bf16[1,3,1,12,16,128]{5,4,3,0,1,2:T(8,128)(2,1)S(1)}, u32[]{:S(2)}, u32[]{:S(2)}) %collective-permute-start) | collective-permute-done | bytes 147488 | tf_op jit(solution)/shard_map/ppermute | solution.py:132
  17.1 2.4 %collective-permute-done.1 = bf16[1,3,1,12,16,128]{5,4,3,0,1,2:T(8,128)(2,1)S(1)} collective-permute-done((bf16[1,3,1,12,16,128]{5,4,3,0,1,2:T(8,128)(2,1)S(1)}, bf16[1,3,1,12,16,128]{5,4,3,0,1,2:T(8,128)(2,1)S(1)}, u32[]{:S(2)}, u32[]{:S(2)}) %collective-permute-start.1) | collective-permute-done | bytes 147488 | tf_op jit(solution)/shard_map/ppermute | solution.py:132
  19.8 4.8 %all_to_all.78 = bf16[3,1,12,144,128]{4,3,1,0,2:T(8,128)(2,1)S(1)} all-to-all(bf16[3,1,12,144,128]{4,3,1,0,2:T(8,128)(2,1)S(1)} %maximum_maximum_fusion), channel_id=1, replica_groups=mesh['dp'=4,'seq'=4,'grp'=2] {'grp'}, dimensions={2} | all-to-all | bytes 2654208 | tf_op jit(solution)/shard_map/all_to_all | solution.py:154
  24.6 6.1 %all-to-all-start.1 = ((bf16[1,4,12,16,128]{4,3,2,0,1:T(8,128)(2,1)}), bf16[1,4,12,16,128]{4,3,2,0,1:T(8,128)(2,1)S(1)}, u32[]{:S(2)}, u32[]{:S(2)}) async-start(bf16[1,4,12,16,128]{4,3,2,0,1:T(8,128)(2,1)} %bitcast.24), calls=%async_computation.1 | async-start | bytes 393216 | tf_op jit(solution)/shard_map/all_to_all | solution.py:143
  31.0 6.0 %all-to-all-done.1 = bf16[1,4,12,16,128]{4,3,2,0,1:T(8,128)(2,1)S(1)} async-done(((bf16[1,4,12,16,128]{4,3,2,0,1:T(8,128)(2,1)}), bf16[1,4,12,16,128]{4,3,2,0,1:T(8,128)(2,1)S(1)}, u32[]{:S(2)}, u32[]{:S(2)}) %all-to-all-start.1) | async-done | bytes 196640 | tf_op jit(solution)/shard_map/all_to_all | solution.py:143
  37.0 4.1 %all_to_all.79 = bf16[1,1,12,144,128]{4,3,1,0,2:T(8,128)(2,1)S(1)} all-to-all(bf16[1,1,12,144,128]{4,3,1,0,2:T(8,128)(2,1)S(1)} %maximum_bitcast_fusion.1), channel_id=1, replica_groups=mesh['dp'=4,'seq'=4,'grp'=2] {'grp'}, dimensions={2} | all-to-all | bytes 884736 | tf_op jit(solution)/shard_map/all_to_all | solution.py:155
  41.1 18.7 %while.16 = (s32[]{:T(128)}, bf16[6,288,128]{2,1,0:T(8,128)(2,1)}, bf16[6,288,128]{2,1,0:T(8,128)(2,1)}, bf16[6,288,128]{2,1,0:T(8,128)(2,1)S(1)}, bf16[6,288,12...) while((s32[]{:T(128)}, bf16[6,288,128]{2,1,0:T(8,128)(2,1)}, ...), condition=%wide.region_6.7_spmd, body=%wide.region_2.6_spmd.sunk | while | flops 129290400 | bytes 4506681 | solution.py:163
  41.8 0.9 fusion.112
  44.9 0.9 fusion.112
  48.0 0.9 fusion.112
  54.2 0.9 fusion.112
  59.8 1.4 maximum_bitcast_fusion
  61.2 1.4 copy.74
  62.5 5.2 %all_to_all.80 = bf16[4,1,6,288,128]{4,0,2,1,3:T(4,128)(2,1)S(1)} all-to-all(bf16[4,1,6,288,128]{4,0,2,1,3:T(4,128)(2,1)S(1)} %copy.74), channel_id=1, replica_groups=mesh['dp'=4,'seq'=4,'grp'=2] {'grp'}, dimensions={3} | all-to-all | bytes 3538944 | tf_op jit(solution)/shard_map/all_to_all | solution.py:176
  68.1 1.5 %copy.76 = bf16[4,1,12,64,128]{4,2,1,0,3:T(8,128)(2,1)} copy(bf16[4,1,12,64,128]{4,3,1,0,2:T(8,128)(2,1)S(1)} %slice.80) | data formatting | bytes 1572864 | tf_op jit(solution)/shard_map/slice | solution.py:178
  69.6 5.0 %all-to-all-start.4 = ((bf16[4,1,12,64,128]{4,2,1,0,3:T(8,128)(2,1)}), bf16[4,1,12,64,128]{4,2,1,0,3:T(8,128)(2,1)S(1)}, u32[]{:S(2)}, u32[]{:S(2)}) async-start(bf16[4,1,12,64,128]{4,2,1,0,3:T(8,128)(2,1)} %copy.76), calls=%async_computation.4 | async-start | bytes 2097152 | tf_op jit(solution)/shard_map/all_to_all | solution.py:177
  74.6 2.2 %fusion.47 = (f32[2,128]{1,0:T(2,128)}, f32[2,12,80]{2,0,1:T(2,128)S(1)}) fusion(f32[2,12,80]{2,0,1:T(2,128)} %copy-done.5, bf16[4,1,12,144,128]{4,3,1,0,2:T(8,128)(2,1)S(1)} %bitcast.144, f32[2,128]{1,0:T(2,128)} %copy-done.9, bf16[3,1,12,80,128]{4,3,2,1,0:T(8,128)(2,1)S(1)} %copy-done), kind=kLoop, calls=%fused_computation.60 | loop fusion | flops 1963904 | bytes 1000448 | tf_op jit(solution)/shard_map/reduce_sum | solution.py:89
  79.3 18.4 %all-to-all-done.4 = bf16[4,1,12,64,128]{4,2,1,0,3:T(8,128)(2,1)S(1)} async-done(((bf16[4,1,12,64,128]{4,2,1,0,3:T(8,128)(2,1)}), bf16[4,1,12,64,128]{4,2,1,0,3:T(8,128)(2,1)S(1)}, u32[]{:S(2)}, u32[]{:S(2)}) %all-to-all-start.4) | async-done | bytes 786464 | tf_op jit(solution)/shard_map/all_to_all | solution.py:177
  99.4 42.7 %psum.7 = f32[2,2,128]{2,1,0:T(2,128)S(1)} all-reduce(f32[2,2,128]{2,1,0:T(2,128)S(1)} %pad_maximum_fusion.3), channel_id=1, replica_groups=mesh['dp'=4,'seq'=4,'grp'=2] {'dp','seq','grp'}, use_global_device_ids=true, to_apply=%region_11.12 | all-reduce | flops 512 | bytes 4096 | tf_op jit(solution)/shard_map/psum | solution.py:184
  (117 shorter events, 24.6 us)
Async XLA Ops:
  0.6 10.9 %copy-start = (bf16[3,1,12,80,128]{4,3,2,1,0:T(8,128)(2,1)S(1)}, bf16[3,1,12,80,128]{4,3,2,1,0:T(8,128)(2,1)}, u32[]{:S(2)}) copy-start(bf16[3,1,12,80,128]{4,3,2,1,0:T(8,128)(2,1)} %param.9) | copy-start | bytes 2211844
  3.7 8.4 %copy-start.9 = (f32[2,128]{1,0:T(2,128)}, f32[2,128]{1,0:T(2,128)S(1)}, u32[]{:S(2)}) copy-start(f32[2,128]{1,0:T(2,128)S(1)} %get-tuple-element.123) | copy-start | bytes 3076
  3.7 9.3 %copy-start.7 = (f32[2,128]{1,0:T(2,128)}, f32[2,128]{1,0:T(2,128)S(1)}, u32[]{:S(2)}) copy-start(f32[2,128]{1,0:T(2,128)S(1)} %get-tuple-element.122) | copy-start | bytes 3076
  3.7 9.3 %copy-start.2 = (f32[2,4,12,16]{3,2,1,0:T(8,128)}, f32[2,4,12,16]{3,2,1,0:T(8,128)S(1)}, u32[]{:S(2)}) copy-start(f32[2,4,12,16]{3,2,1,0:T(8,128)S(1)} %add_rsqrt_fusion) | copy-start | bytes 18436
  5.1 14.4 %collective-permute-start.2 = (bf16[1,3,1,12,16,128]{5,4,3,0,1,2:T(8,128)(2,1)S(1)}, bf16[1,3,1,12,16,128]{5,4,3,0,1,2:T(8,128)(2,1)S(1)}, u32[]{:S(2)}, u32[]{:S(2)}) collective-permute-start(bf16[1,3,1,12,16,128]{5,4,3,0,1,2:T(8,128)(2,1)S(1)} %get-tuple-element.119), channel_id=1, source_target_pairs={{0,6},{2,0},{4,2},{6,4},{1,7},{3,1},{5,3},{7,5},{8,14},{10,8},{12,... | collective-permute-start | bytes 442376 | tf_op jit(solution)/shard_map/ppermute | solution.py:132
  5.6 11.5 %collective-permute-start = (bf16[1,3,1,12,16,128]{5,4,3,0,1,2:T(8,128)(2,1)S(1)}, bf16[1,3,1,12,16,128]{5,4,3,0,1,2:T(8,128)(2,1)S(1)}, u32[]{:S(2)}, u32[]{:S(2)}) collective-permute-start(bf16[1,3,1,12,16,128]{5,4,3,0,1,2:T(8,128)(2,1)S(1)} %get-tuple-element.120), channel_id=1, source_target_pairs={{0,2},{2,4},{4,6},{6,0},{1,3},{3,5},{5,7},{7,1},{8,10},{10,12},{12... | collective-permute-start | bytes 442376 | tf_op jit(solution)/shard_map/ppermute | solution.py:132
  7.2 12.3 %collective-permute-start.1 = (bf16[1,3,1,12,16,128]{5,4,3,0,1,2:T(8,128)(2,1)S(1)}, bf16[1,3,1,12,16,128]{5,4,3,0,1,2:T(8,128)(2,1)S(1)}, u32[]{:S(2)}, u32[]{:S(2)}) collective-permute-start(bf16[1,3,1,12,16,128]{5,4,3,0,1,2:T(8,128)(2,1)S(1)} %get-tuple-element.121), channel_id=1, source_target_pairs={{0,4},{2,6},{4,0},{6,2},{1,5},{3,7},{5,1},{7,3},{8,12},{10,14},{12... | collective-permute-start | bytes 442376 | tf_op jit(solution)/shard_map/ppermute | solution.py:132
  12.1 0.6 copy-start.5
  24.6 12.4 %all-to-all-start.1 = ((bf16[1,4,12,16,128]{4,3,2,0,1:T(8,128)(2,1)}), bf16[1,4,12,16,128]{4,3,2,0,1:T(8,128)(2,1)S(1)}, u32[]{:S(2)}, u32[]{:S(2)}) async-start(bf16[1,4,12,16,128]{4,3,2,0,1:T(8,128)(2,1)} %bitcast.24), calls=%async_computation.1 | async-start | bytes 393216 | tf_op jit(solution)/shard_map/all_to_all | solution.py:143
  30.8 6.1 %copy-start.4 = (bf16[1,12,80,128]{3,2,1,0:T(8,128)(2,1)S(1)}, bf16[1,12,80,128]{3,2,1,0:T(8,128)(2,1)}, u32[]{:S(2)}) copy-start(bf16[1,12,80,128]{3,2,1,0:T(8,128)(2,1)} %param.11) | copy-start | bytes 737284
  69.6 28.0 %all-to-all-start.4 = ((bf16[4,1,12,64,128]{4,2,1,0,3:T(8,128)(2,1)}), bf16[4,1,12,64,128]{4,2,1,0,3:T(8,128)(2,1)S(1)}, u32[]{:S(2)}, u32[]{:S(2)}) async-start(bf16[4,1,12,64,128]{4,2,1,0,3:T(8,128)(2,1)} %copy.76), calls=%async_computation.4 | async-start | bytes 2097152 | tf_op jit(solution)/shard_map/all_to_all | solution.py:177
  74.6 2.9 %copy-start.6 = (f32[2,12,80]{2,0,1:T(2,128)S(1)}, f32[2,12,80]{2,0,1:T(2,128)}, u32[]{:S(2)}) copy-start(f32[2,12,80]{2,0,1:T(2,128)} %copy-done.5) | copy-start | bytes 23044
  74.6 2.9 %copy-start.10 = (f32[2,128]{1,0:T(2,128)S(1)}, f32[2,128]{1,0:T(2,128)}, u32[]{:S(2)}) copy-start(f32[2,128]{1,0:T(2,128)} %copy-done.9) | copy-start | bytes 3076
  78.3 19.9 %copy-start.1 = (bf16[3,4,12,16,128]{4,3,2,1,0:T(8,128)(2,1)S(1)}, bf16[3,4,12,16,128]{4,3,2,1,0:T(8,128)(2,1)}, u32[]{:S(2)}) copy-start(bf16[3,4,12,16,128]{4,3,2,1,0:T(8,128)(2,1)} %param.8) | copy-start | bytes 1769476
  78.3 19.9 %copy-start.3 = (f32[2,4,12,16]{3,2,1,0:T(8,128)S(1)}, f32[2,4,12,16]{3,2,1,0:T(8,128)}, u32[]{:S(2)}) copy-start(f32[2,4,12,16]{3,2,1,0:T(8,128)} %copy-done.2) | copy-start | bytes 18436
  78.3 19.9 %copy-start.8 = (f32[2,128]{1,0:T(2,128)S(1)}, f32[2,128]{1,0:T(2,128)}, u32[]{:S(2)}) copy-start(f32[2,128]{1,0:T(2,128)} %copy-done.7) | copy-start | bytes 3076
  97.7 1.8 %copy-start.11 = (f32[2,128]{1,0:T(2,128)S(1)}, f32[2,128]{1,0:T(2,128)}, u32[]{:S(2)}) copy-start(f32[2,128]{1,0:T(2,128)} %get-tuple-element.84) | copy-start | bytes 3076
